TPU v7x, 64 devices: a 2x2x8 block of a 4x4x8 slice. The times are simulated.
64 devices in a mesh: dp: 4 (over x, y), ep: 16 (over z, core).
Axes of the slice: x: 2, y: 2, z: 8, core: 2. Of those that a mesh axis runs over, the one named last changes fastest.
The devices are a block of a 4x4x8 slice.
Arguments:
- tokens_a: bfloat16 [4096, 1024], P(('dp', 'ep')), parts along dimension 0
- experts_a: int32 [4096, 8], P(('dp', 'ep')), parts along dimension 0
- slots_a: int32 [4096, 8], P(('dp', 'ep')), parts along dimension 0
- gates_a: bfloat16 [4096, 8], P(('dp', 'ep')), parts along dimension 0
- tokens_b: bfloat16 [4096, 1024], P(('dp', 'ep')), parts along dimension 0
- experts_b: int32 [4096, 8], P(('dp', 'ep')), parts along dimension 0
- slots_b: int32 [4096, 8], P(('dp', 'ep')), parts along dimension 0
- gates_b: bfloat16 [4096, 8], P(('dp', 'ep')), parts along dimension 0
- attn_gain: bfloat16 [1024], replicated
- w_query: bfloat16 [1024, 16, 64], replicated
- w_key: bfloat16 [1024, 16, 64], replicated
- w_value: bfloat16 [1024, 16, 64], replicated
- w_out: bfloat16 [16, 64, 1024], replicated
- moe_gain: bfloat16 [1024], replicated
- w_gate: bfloat16 [32, 1024, 512], P('ep')
- w_up: bfloat16 [32, 1024, 512], P('ep')
- w_down: bfloat16 [32, 512, 1024], P('ep')
Outputs:
- output 1: bfloat16 [4096, 1024], P(('dp', 'ep')), parts along dimension 0
- output 2: bfloat16 [4096, 1024], P(('dp', 'ep')), parts along dimension 0
There are 4 independent parts. A program takes and returns all parts, laid end to end along the dimension named above; an argument that names none is the same for every part.
All inputs are finite; a program needn't handle non-finite values.
Results may differ from a plain program's by a relative error of at most 0.014492.
Values are sent between devices in bfloat16 or wider.
A program may use at most 768 MiB of HBM per device.

v0:
```python
import jax
import jax.numpy as jnp
from jax import lax
from jax.sharding import PartitionSpec as P

NORM_EPS = 1e-6
MASK_VALUE = -1e30


def rms_norm(rows, gain_vec):
    rows_f = rows.astype(jnp.float32)
    inv_rms = lax.rsqrt(jnp.mean(rows_f * rows_f, axis=-1, keepdims=True) + NORM_EPS)
    return (rows_f * inv_rms * gain_vec.astype(jnp.float32)).astype(jnp.bfloat16)


def attention_block(sequence, attn_gain, w_query, w_key, w_value, w_out):
    seq_len = sequence.shape[0]
    normed = rms_norm(sequence, attn_gain)
    query = jnp.einsum("td,dhe->the", normed, w_query, preferred_element_type=jnp.float32).astype(jnp.bfloat16)
    keys = jnp.einsum("td,dhe->the", normed, w_key, preferred_element_type=jnp.float32).astype(jnp.bfloat16)
    values = jnp.einsum("td,dhe->the", normed, w_value, preferred_element_type=jnp.float32).astype(jnp.bfloat16)
    scores = jnp.einsum("qhe,khe->hqk", query, keys, preferred_element_type=jnp.float32) * (w_query.shape[2] ** -0.5)
    causal = lax.broadcasted_iota(jnp.int32, (seq_len, seq_len), 0) >= lax.broadcasted_iota(jnp.int32, (seq_len, seq_len), 1)
    scores = jnp.where(causal[None, :, :], scores, MASK_VALUE)
    attn_prob = jax.nn.softmax(scores, axis=-1).astype(jnp.bfloat16)
    context = jnp.einsum("hqk,khe->qhe", attn_prob, values, preferred_element_type=jnp.float32).astype(jnp.bfloat16)
    attn_out = jnp.einsum("qhe,hed->qd", context, w_out, preferred_element_type=jnp.float32)
    return (sequence.astype(jnp.float32) + attn_out).astype(jnp.bfloat16)


def capacity_of(seq_len, top_k, experts_total):
    return 8 * max(1, (seq_len * top_k) // (4 * experts_total))


def dispatch_rows(normed, dest_row, experts_total, capacity):
    seq_len, model_dim = normed.shape
    top_k = dest_row.shape[0] // seq_len
    token_of = jnp.arange(seq_len * top_k, dtype=jnp.int32) // top_k
    source = jnp.full((experts_total * capacity,), seq_len, jnp.int32).at[dest_row].set(token_of, mode="drop")
    return jnp.take(normed, source, axis=0, mode="fill", fill_value=0).reshape(experts_total, capacity, model_dim)


def combine_rows(residual, returned, dest_row, gates):
    seq_len, model_dim = residual.shape
    top_k = gates.shape[1]
    picked = jnp.take(returned.reshape(-1, model_dim), dest_row, axis=0, mode="fill", fill_value=0).reshape(seq_len, top_k, model_dim)
    mixed_sum = jnp.einsum("tk,tkd->td", gates, picked, preferred_element_type=jnp.float32)
    return (residual.astype(jnp.float32) + mixed_sum).astype(jnp.bfloat16)


def expert_ffn(received, w_gate, w_up, w_down):
    gate_act = jnp.einsum("pecd,edf->pecf", received, w_gate, preferred_element_type=jnp.float32)
    up_act = jnp.einsum("pecd,edf->pecf", received, w_up, preferred_element_type=jnp.float32)
    hidden = (jax.nn.silu(gate_act) * up_act).astype(jnp.bfloat16)
    return jnp.einsum("pecf,efd->pecd", hidden, w_down, preferred_element_type=jnp.float32).astype(jnp.bfloat16)


def moe_layer(tokens, experts, slots, gates, attn_gain, w_query, w_key, w_value, w_out, moe_gain, w_gate, w_up, w_down, group):
    seq_len, model_dim = tokens.shape
    local_experts = w_gate.shape[0]
    experts_total = local_experts * group
    capacity = capacity_of(seq_len, experts.shape[1], experts_total)
    residual = attention_block(tokens, attn_gain, w_query, w_key, w_value, w_out)
    normed = rms_norm(residual, moe_gain)
    dest_row = jnp.where(slots >= 0, experts * capacity + slots, experts_total * capacity).reshape(-1)
    dispatched = dispatch_rows(normed, dest_row, experts_total, capacity)
    received = lax.all_to_all(dispatched, "ep", 0, 0, tiled=True).reshape(group, local_experts, capacity, model_dim)
    expert_out = expert_ffn(received, w_gate, w_up, w_down).reshape(experts_total, capacity, model_dim)
    returned = lax.all_to_all(expert_out, "ep", 0, 0, tiled=True)
    return combine_rows(residual, returned, dest_row, gates)


def solution(mesh):
    group = mesh.shape["ep"]
    row_spec = P(("dp", "ep"), None)
    full_spec = P(None, None, None)
    gain_spec = P(None)
    expert_spec = P("ep", None, None)
    in_specs = (row_spec, row_spec, row_spec, row_spec, row_spec, row_spec, row_spec, row_spec, gain_spec, full_spec, full_spec, full_spec, full_spec, gain_spec, expert_spec, expert_spec, expert_spec)

    def device_fn(tokens_a, experts_a, slots_a, gates_a, tokens_b, experts_b, slots_b, gates_b, attn_gain, w_query, w_key, w_value, w_out, moe_gain, w_gate, w_up, w_down):
        out_a = moe_layer(tokens_a, experts_a, slots_a, gates_a, attn_gain, w_query, w_key, w_value, w_out, moe_gain, w_gate, w_up, w_down, group)
        out_b = moe_layer(tokens_b, experts_b, slots_b, gates_b, attn_gain, w_query, w_key, w_value, w_out, moe_gain, w_gate, w_up, w_down, group)
        return out_a, out_b

    return jax.shard_map(device_fn, mesh=mesh, in_specs=in_specs, out_specs=(row_spec, row_spec), check_vma=False)
```

profile of v0, /device:TPU:21, one launch (start us, length us, event | category | flops | bytes accessed | tf_op | source)
XLA Modules:
  0.0 265.9 jit_solution(8096572685782837158)
XLA Ops:
  2.7 3.0 %convolution_convert_fusion.1 = bf16[64,16,64]{2,0,1:T(8,128)(2,1)S(1)} fusion(bf16[1024,16,64]{0,2,1:T(8,128)(2,1)} %param.31, bf16[64,1024]{1,0:T(8,128)(2,1)} %param.25, f32[64]{0:T(128)S(1)} %add_rsqrt_fusion.1, f32[1024]{0:T(1024)S(1)} %convert_element_type.103), kind=kOutput, calls=%fused_computation.51 | convolution fusion | flops 134545408 | bytes 2363648 | tf_op jit(solution)/shard_map/td,dhe->the/dot_general | solution.py:20
  12.0 3.7 %fusion.34 = f32[16,64,64]{1,2,0:T(8,128)} fusion(bf16[64,16,64]{2,0,1:T(8,128)(2,1)S(1)} %convolution_convert_fusion.1, bf16[1024,16,64]{0,2,1:T(8,128)(2,1)} %param.30, pred[64,64]{0,1:T(8,128)(4,1)S(1)} %iota_compare_fusion, bf16[64,1024]{1,0:T(8,128)(2,1)S(1)} %copy-done.3, f32[64]{0:T(128)S(1)} %add_rsqrt_fusion.1, f32[1024]{0:T(1024)S(1)} %convert_element_type.103), kind=kOutput, calls=%fused_computation.47 | convolution fusion | flops 143065088 | bytes 2629888 | tf_op jit(solution)/shard_map/qhe,khe->hqk/dot_general | solution.py:22
  17.3 3.7 %fusion.35 = f32[16,64,64]{1,2,0:T(8,128)} fusion(bf16[64,16,64]{2,0,1:T(8,128)(2,1)S(1)} %convolution_convert_fusion.4, bf16[1024,16,64]{0,2,1:T(8,128)(2,1)} %param.30, pred[64,64]{0,1:T(8,128)(4,1)S(1)} %iota_compare_fusion, bf16[64,1024]{1,0:T(8,128)(2,1)S(1)} %copy-done.4, f32[1024]{0:T(1024)S(1)} %convert_element_type.103, f32[64]{0:T(128)S(1)} %add_rsqrt_fusion.3), kind=kOutput, calls=%fused_computation.49 | convolution fusion | flops 143065088 | bytes 2629888 | tf_op jit(solution)/shard_map/qhe,khe->hqk/dot_general | solution.py:22
  26.1 2.9 %multiply_reduce_fusion.1 = (f32[64]{0:T(128)S(1)}, f32[64,1024]{1,0:T(8,128)S(1)}) fusion(bf16[16,64,1024]{2,1,0:T(8,128)(2,1)} %param.33, bf16[64,16,64]{2,1,0:T(8,128)(2,1)S(1)} %copy-done.7, f32[16,64]{1,0:T(8,128)S(1)} %fusion.123, f32[16,64,64]{1,2,0:T(8,128)} %fusion.35, bf16[64,1024]{1,0:T(8,128)(2,1)S(1)} %copy-done.4), kind=kOutput, calls=%fused_computation.104 | convolution fusion | flops 143262720 | bytes 2887936 | tf_op jit(solution)/shard_map/qhe,hed->qd/dot_general | solution.py:27
  29.1 5.4 %gather_fusion.2 = bf16[1024,1024]{1,0:T(8,128)(2,1)} fusion(bf16[64,1024]{1,0:T(8,128)(2,1)S(1)} %get-tuple-element.4, s32[1024]{0:T(1024)S(1)} %fusion.97), kind=kCustom, calls=%fused_computation.2.clone | custom fusion | bytes 4198400 | tf_op jit(solution)/shard_map/jit(_take)/gather | solution.py:40
  34.4 3.2 %broadcast_select_fusion = bf16[1024,1024]{1,0:T(8,128)(2,1)} fusion(bf16[1024,1024]{1,0:T(8,128)(2,1)} %gather_fusion.2, pred[1024]{0:T(1024)(128)(4,1)S(1)} %compare_and_fusion), kind=kLoop, calls=%fused_computation.36 | loop fusion | flops 1048576 | bytes 4195328 | tf_op jit(solution)/shard_map/jit(_take)/select_n | solution.py:40
  37.6 10.9 %all-to-all-start.2 = ((bf16[32,32,1024]{2,1,0:T(8,128)(2,1)}), bf16[32,32,1024]{2,1,0:T(8,128)(2,1)}, u32[]{:S(2)}, u32[]{:S(2)}) async-start(bf16[32,32,1024]{2,1,0:T(8,128)(2,1)} %bitcast.173), calls=%async_computation.2 | async-start | bytes 4194304 | tf_op jit(solution)/shard_map/all_to_all | solution.py:67
  51.2 5.4 %gather_fusion = bf16[1024,1024]{1,0:T(8,128)(2,1)} fusion(bf16[64,1024]{1,0:T(8,128)(2,1)S(1)} %get-tuple-element.5, s32[1024]{0:T(1024)S(1)} %fusion.96), kind=kCustom, calls=%fused_computation.clone | custom fusion | bytes 4198400 | tf_op jit(solution)/shard_map/jit(_take)/gather | solution.py:40
  56.6 3.2 %broadcast_select_fusion.1 = bf16[1024,1024]{1,0:T(8,128)(2,1)} fusion(bf16[1024,1024]{1,0:T(8,128)(2,1)} %gather_fusion, pred[1024]{0:T(1024)(128)(4,1)S(1)} %compare_and_fusion.1), kind=kLoop, calls=%fused_computation.37 | loop fusion | flops 1048576 | bytes 4195328 | tf_op jit(solution)/shard_map/jit(_take)/select_n | solution.py:40
  59.8 37.5 %all-to-all-done.2 = bf16[32,32,1024]{2,1,0:T(8,128)(2,1)} async-done(((bf16[32,32,1024]{2,1,0:T(8,128)(2,1)}), bf16[32,32,1024]{2,1,0:T(8,128)(2,1)}, u32[]{:S(2)}, u32[]{:S(2)}) %all-to-all-start.2) | async-done | bytes 2097184 | tf_op jit(solution)/shard_map/all_to_all | solution.py:67
  97.3 5.4 %all-to-all-start = ((bf16[32,32,1024]{2,1,0:T(8,128)(2,1)}), bf16[32,32,1024]{2,1,0:T(8,128)(2,1)}, u32[]{:S(2)}, u32[]{:S(2)}) async-start(bf16[32,32,1024]{2,1,0:T(8,128)(2,1)} %bitcast.174), calls=%async_computation | async-start | bytes 4194304 | tf_op jit(solution)/shard_map/all_to_all | solution.py:67
  102.7 4.8 %fusion.7 = f32[2,16,32,512]{3,2,1,0:T(8,128)} fusion(bf16[2,1024,512]{2,1,0:T(8,128)(2,1)} %param.36, bf16[16,2,32,1024]{3,2,1,0:T(8,128)(2,1)} %bitcast.25), kind=kOutput, calls=%fused_computation.14 | convolution fusion | flops 1073741824 | bytes 6291456 | tf_op jit(solution)/shard_map/pecd,edf->pecf/dot_general | solution.py:53
  107.5 6.7 %convert_bitcast_fusion = bf16[16,2,32,1024]{3,2,0,1:T(8,128)(2,1)} fusion(bf16[2,512,1024]{2,1,0:T(8,128)(2,1)S(1)} %copy-done, f32[2,16,32,512]{3,2,1,0:T(8,128)} %fusion.7, bf16[2,1024,512]{2,1,0:T(8,128)(2,1)} %param.35, bf16[16,2,32,1024]{3,2,1,0:T(8,128)(2,1)} %bitcast.25), kind=kOutput, calls=%fused_computation.34 | convolution fusion | flops 2151677952 | bytes 10485760 | tf_op jit(solution)/shard_map/pecf,efd->pecd/dot_general | solution.py:55
  114.2 3.2 %copy.26 = bf16[16,2,32,1024]{3,2,1,0:T(8,128)(2,1)} copy(bf16[16,2,32,1024]{3,2,0,1:T(8,128)(2,1)} %convert_bitcast_fusion) | data formatting | bytes 4194304 | tf_op jit(solution)/shard_map/convert_element_type | solution.py:55
  117.4 34.1 %all-to-all-done = bf16[32,32,1024]{2,1,0:T(8,128)(2,1)} async-done(((bf16[32,32,1024]{2,1,0:T(8,128)(2,1)}), bf16[32,32,1024]{2,1,0:T(8,128)(2,1)}, u32[]{:S(2)}, u32[]{:S(2)}) %all-to-all-start) | async-done | bytes 2097184 | tf_op jit(solution)/shard_map/all_to_all | solution.py:67
  151.5 5.5 %all-to-all-start.3 = ((bf16[32,32,1024]{2,1,0:T(8,128)(2,1)}), bf16[32,32,1024]{2,1,0:T(8,128)(2,1)}, u32[]{:S(2)}, u32[]{:S(2)}) async-start(bf16[32,32,1024]{2,1,0:T(8,128)(2,1)} %bitcast.176), calls=%async_computation.3 | async-start | bytes 4194304 | tf_op jit(solution)/shard_map/all_to_all | solution.py:69
  157.0 4.9 %fusion.9 = f32[2,16,32,512]{3,2,1,0:T(8,128)} fusion(bf16[2,1024,512]{2,1,0:T(8,128)(2,1)} %param.36, bf16[16,2,32,1024]{3,2,1,0:T(8,128)(2,1)} %bitcast.5), kind=kOutput, calls=%fused_computation.16 | convolution fusion | flops 1073741824 | bytes 6291456 | tf_op jit(solution)/shard_map/pecd,edf->pecf/dot_general | solution.py:53
  161.8 6.7 %convert_bitcast_fusion.1 = bf16[16,2,32,1024]{3,2,0,1:T(8,128)(2,1)} fusion(bf16[2,512,1024]{2,1,0:T(8,128)(2,1)S(1)} %copy-done, f32[2,16,32,512]{3,2,1,0:T(8,128)} %fusion.9, bf16[2,1024,512]{2,1,0:T(8,128)(2,1)} %param.35, bf16[16,2,32,1024]{3,2,1,0:T(8,128)(2,1)} %bitcast.5), kind=kOutput, calls=%fused_computation.35 | convolution fusion | flops 2151677952 | bytes 10485760 | tf_op jit(solution)/shard_map/pecf,efd->pecd/dot_general | solution.py:55
  168.6 3.2 %copy.22 = bf16[16,2,32,1024]{3,2,1,0:T(8,128)(2,1)} copy(bf16[16,2,32,1024]{3,2,0,1:T(8,128)(2,1)} %convert_bitcast_fusion.1) | data formatting | bytes 4194304 | tf_op jit(solution)/shard_map/convert_element_type | solution.py:55
  171.8 34.0 %all-to-all-done.3 = bf16[32,32,1024]{2,1,0:T(8,128)(2,1)} async-done(((bf16[32,32,1024]{2,1,0:T(8,128)(2,1)}), bf16[32,32,1024]{2,1,0:T(8,128)(2,1)}, u32[]{:S(2)}, u32[]{:S(2)}) %all-to-all-start.3) | async-done | bytes 2097184 | tf_op jit(solution)/shard_map/all_to_all | solution.py:69
  205.8 5.6 %all-to-all-start.1 = ((bf16[32,32,1024]{2,1,0:T(8,128)(2,1)}), bf16[32,32,1024]{2,1,0:T(8,128)(2,1)}, u32[]{:S(2)}, u32[]{:S(2)}) async-start(bf16[32,32,1024]{2,1,0:T(8,128)(2,1)} %bitcast.175), calls=%async_computation.1 | async-start | bytes 4194304 | tf_op jit(solution)/shard_map/all_to_all | solution.py:69
  211.8 4.6 %gather_fusion.3 = bf16[512,1024]{1,0:T(8,128)(2,1)S(1)} fusion(bf16[1024,1024]{1,0:T(8,128)(2,1)} %bitcast.33, s32[1024]{0:T(1024)S(1)} %pad_clamp_fusion), kind=kCustom, calls=%fused_computation.3.clone | custom fusion | bytes 2099200 | tf_op jit(solution)/shard_map/jit(_take)/gather | solution.py:46
  218.1 42.1 %all-to-all-done.1 = bf16[32,32,1024]{2,1,0:T(8,128)(2,1)} async-done(((bf16[32,32,1024]{2,1,0:T(8,128)(2,1)}), bf16[32,32,1024]{2,1,0:T(8,128)(2,1)}, u32[]{:S(2)}, u32[]{:S(2)}) %all-to-all-start.1) | async-done | bytes 2097184 | tf_op jit(solution)/shard_map/all_to_all | solution.py:69
  260.1 4.6 %gather_fusion.1 = bf16[512,1024]{1,0:T(8,128)(2,1)S(1)} fusion(bf16[1024,1024]{1,0:T(8,128)(2,1)} %bitcast.16, s32[1024]{0:T(1024)S(1)} %pad_clamp_fusion.1), kind=kCustom, calls=%fused_computation.1.clone | custom fusion | bytes 2099200 | tf_op jit(solution)/shard_map/jit(_take)/gather | solution.py:46
  (76 shorter events, 20.9 us)
Async XLA Ops:
  0.6 106.9 %copy-start = (bf16[2,512,1024]{2,1,0:T(8,128)(2,1)S(1)}, bf16[2,512,1024]{2,1,0:T(8,128)(2,1)}, u32[]{:S(2)}) copy-start(bf16[2,512,1024]{2,1,0:T(8,128)(2,1)} %param.37) | copy-start | bytes 6291460
  0.6 5.0 %copy-start.3 = (bf16[64,1024]{1,0:T(8,128)(2,1)S(1)}, bf16[64,1024]{1,0:T(8,128)(2,1)}, u32[]{:S(2)}) copy-start(bf16[64,1024]{1,0:T(8,128)(2,1)} %param.25) | copy-start | bytes 393220
  0.7 5.0 %copy-start.2 = (bf16[1024,16,64]{0,2,1:T(8,128)(2,1)S(1)}, bf16[1024,16,64]{0,2,1:T(8,128)(2,1)}, u32[]{:S(2)}) copy-start(bf16[1024,16,64]{0,2,1:T(8,128)(2,1)} %param.32) | copy-start | bytes 6291460
  2.7 4.2 %copy-start.4 = (bf16[64,1024]{1,0:T(8,128)(2,1)S(1)}, bf16[64,1024]{1,0:T(8,128)(2,1)}, u32[]{:S(2)}) copy-start(bf16[64,1024]{1,0:T(8,128)(2,1)} %param.21) | copy-start | bytes 393220
  2.7 4.3 %copy-start.1 = (bf16[1024,16,64]{0,2,1:T(8,128)(2,1)S(1)}, bf16[1024,16,64]{0,2,1:T(8,128)(2,1)}, u32[]{:S(2)}) copy-start(bf16[1024,16,64]{0,2,1:T(8,128)(2,1)} %param.31) | copy-start | bytes 6291460
  7.0 2.3 copy-start.8
  7.0 2.3 copy-start.9
  17.3 5.9 %copy-start.12 = (bf16[1024]{0:T(1024)(128)(2,1)S(1)}, bf16[1024]{0:T(1024)(128)(2,1)}, u32[]{:S(2)}) copy-start(bf16[1024]{0:T(1024)(128)(2,1)} %param.34) | copy-start | bytes 6148
  23.2 2.8 %copy-start.7 = (bf16[64,16,64]{2,1,0:T(8,128)(2,1)S(1)}, bf16[64,16,64]{2,1,0:T(8,128)(2,1)}, u32[]{:S(2)}) copy-start(bf16[64,16,64]{2,1,0:T(8,128)(2,1)} %copy.65) | copy-start | bytes 393220
  26.0 2.9 %copy-start.5 = (f32[64,1024]{1,0:T(8,128)}, f32[64,1024]{1,0:T(8,128)S(1)}, u32[]{:S(2)}) copy-start(f32[64,1024]{1,0:T(8,128)S(1)} %get-tuple-element.7) | copy-start | bytes 786436
  37.6 10.9 %copy-start.10 = (s32[64,8]{0,1:T(8,128)S(1)}, s32[64,8]{0,1:T(8,128)}, u32[]{:S(2)}) copy-start(s32[64,8]{0,1:T(8,128)} %param.23) | copy-start | bytes 6148
  37.6 10.9 %copy-start.11 = (s32[64,8]{0,1:T(8,128)S(1)}, s32[64,8]{0,1:T(8,128)}, u32[]{:S(2)}) copy-start(s32[64,8]{0,1:T(8,128)} %param.22) | copy-start | bytes 6148
  37.6 59.7 %all-to-all-start.2 = ((bf16[32,32,1024]{2,1,0:T(8,128)(2,1)}), bf16[32,32,1024]{2,1,0:T(8,128)(2,1)}, u32[]{:S(2)}, u32[]{:S(2)}) async-start(bf16[32,32,1024]{2,1,0:T(8,128)(2,1)} %bitcast.173), calls=%async_computation.2 | async-start | bytes 4194304 | tf_op jit(solution)/shard_map/all_to_all | solution.py:67
  97.3 54.2 %all-to-all-start = ((bf16[32,32,1024]{2,1,0:T(8,128)(2,1)}), bf16[32,32,1024]{2,1,0:T(8,128)(2,1)}, u32[]{:S(2)}, u32[]{:S(2)}) async-start(bf16[32,32,1024]{2,1,0:T(8,128)(2,1)} %bitcast.174), calls=%async_computation | async-start | bytes 4194304 | tf_op jit(solution)/shard_map/all_to_all | solution.py:67
  151.5 54.3 %all-to-all-start.3 = ((bf16[32,32,1024]{2,1,0:T(8,128)(2,1)}), bf16[32,32,1024]{2,1,0:T(8,128)(2,1)}, u32[]{:S(2)}, u32[]{:S(2)}) async-start(bf16[32,32,1024]{2,1,0:T(8,128)(2,1)} %bitcast.176), calls=%async_computation.3 | async-start | bytes 4194304 | tf_op jit(solution)/shard_map/all_to_all | solution.py:69
  205.8 5.7 %copy-start.13 = (bf16[64,8]{0,1:T(8,128)(2,1)S(1)}, bf16[64,8]{0,1:T(8,128)(2,1)}, u32[]{:S(2)}) copy-start(bf16[64,8]{0,1:T(8,128)(2,1)} %param.28) | copy-start | bytes 3076
  205.8 5.9 %copy-start.14 = (bf16[64,8]{0,1:T(8,128)(2,1)S(1)}, bf16[64,8]{0,1:T(8,128)(2,1)}, u32[]{:S(2)}) copy-start(bf16[64,8]{0,1:T(8,128)(2,1)} %param.24) | copy-start | bytes 3076
  205.8 54.4 %all-to-all-start.1 = ((bf16[32,32,1024]{2,1,0:T(8,128)(2,1)}), bf16[32,32,1024]{2,1,0:T(8,128)(2,1)}, u32[]{:S(2)}, u32[]{:S(2)}) async-start(bf16[32,32,1024]{2,1,0:T(8,128)(2,1)} %bitcast.175), calls=%async_computation.1 | async-start | bytes 4194304 | tf_op jit(solution)/shard_map/all_to_all | solution.py:69
  216.4 1.0 copy-start.6
where the time goes:
time: 267 us; the launch traced here: 266 us
  waiting for transfers between devices  148 us (55%)
  matrix products  43.7 us (16%)
  local copies, waits for them, and re-layouts  33.5 us (13%)
  starting transfers between devices  27.3 us (10%)
  other arithmetic  12.8 us (5%)
    all_to_all x2, waiting for transfers between devices, moe_layer(): returned = lax.all_to_all(expert_out, 'ep', 0, 0, tiled=True)  76 us
    all_to_all x2, waiting for transfers between devices, moe_layer(): lax.all_to_all(dispatched, 'ep', 0, 0, tiled=True)  71.6 us
    all_to_all x2, starting transfers between devices, moe_layer(): lax.all_to_all(dispatched, 'ep', 0, 0, tiled=True)  16.3 us
    dot_general x2, matrix products, expert_ffn(): jnp.einsum('pecf,efd->pecd', hidden, w_down, preferred_element_type=jnp.f...  13.5 us
    all_to_all x2, starting transfers between devices, moe_layer(): returned = lax.all_to_all(expert_out, 'ep', 0, 0, tiled=True)  11 us
    gather x2, local copies, waits for them, and re-layouts, dispatch_rows(): jnp.take(normed, source, axis=0, mode='fill', fill_value=0)  10.8 us
    dot_general x2, matrix products, expert_ffn(): jnp.einsum('pecd,edf->pecf', received, w_up, preferred_element_type=jnp.f...  9.68 us
    gather x2, local copies, waits for them, and re-layouts, combine_rows(): jnp.take(returned.reshape(-1, model_dim), dest_row, axis=0, mode='fill',...  9.18 us
  transfers between devices with their start and end apart: 4, of which 4 were waited for; matrix products, arithmetic and copies ran while one was open for 18% of the time, Pallas kernels for 0%

commit v1 on v0

v1 whole, which is shorter than its diff:
```python
import functools

import jax
import jax.numpy as jnp
from jax import lax
from jax.experimental import pallas as pl
from jax.experimental.pallas import tpu as pltpu
from jax.sharding import PartitionSpec as P

NORM_EPS = 1e-6
MASK_VALUE = -1e30
LANES = 128
PIECES = 1
MESH = pl.DeviceIdType.MESH
NT = (((1,), (1,)), ((), ()))
TN = (((0,), (0,)), ((), ()))
F32 = jnp.float32
BF16 = jnp.bfloat16


def layer_kernel(
    group,
    tok_a, exp_a, slot_a, gate_a, tok_b, exp_b, slot_b, gate_b, attn_gain, wq_h, wk_h, wv_h, wo_h, moe_gain, wg_h, wu_h, wd_h,
    out_a, out_b,
    x_ref, exp_ref, slot_ref, gate_ref, again_ref, mgain_ref, wq, wk, wv, wo, wg, wu, wd,
    a_ref, q_ref, k_ref, v_ref, c_ref, h_ref, usend, uown, ulr, ufar, sel_ref, wbuf, hid_ref,
    part, pfar, pown, rbuf, fin, ownr, out_ref,
    lsem, ssem, wrecv, orecv, agrecv, rsrecv, finrecv,
):
    seq, dim = tok_a.shape
    both = 2 * seq
    blocks = dim // LANES
    urows = blocks * seq
    local = wg_h.shape[0]
    experts = 2 * local
    ffn = wg_h.shape[2]
    top_k = exp_a.shape[0]
    chips = group // 2
    half = chips // 2
    gw_rows = local * group // 2

    me = lax.axis_index("ep")
    z = lax.div(me, 2)
    core = lax.rem(me, 2)
    other = 1 - core
    sibling = 2 * z + other
    right = lax.rem(z + 1, chips)
    left = lax.rem(z + chips - 1, chips)
    toward = (right, left)

    barrier = pltpu.get_barrier_semaphore()
    for peer in (2 * left, 2 * left + 1, 2 * right, 2 * right + 1, sibling):
        pl.semaphore_signal(barrier, inc=1, device_id={"ep": peer}, device_id_type=MESH)

    sends = []

    def local_copy(i, src, dst):
        copy = pltpu.make_async_copy(src, dst, lsem.at[i])
        copy.start()
        return copy

    def remote(src, dst, rsem, peer):
        copy = pltpu.make_async_remote_copy(
            src_ref=src, dst_ref=dst, send_sem=ssem.at[len(sends)], recv_sem=rsem, device_id={"ep": peer}, device_id_type=MESH
        )
        copy.start()
        sends.append(copy)

    def arrived(dst, rsem):
        pltpu.make_async_remote_copy(
            src_ref=dst, dst_ref=dst, send_sem=ssem.at[0], recv_sem=rsem, device_id={"ep": sibling}, device_id_type=MESH
        ).wait_recv()

    small = [
        local_copy(0, tok_a, x_ref.at[pl.ds(0, seq)]),
        local_copy(1, tok_b, x_ref.at[pl.ds(seq, seq)]),
        local_copy(2, attn_gain, again_ref),
        local_copy(3, moe_gain, mgain_ref),
    ]
    loads = [local_copy(4, wq_h, wq), local_copy(5, wk_h, wk), local_copy(6, wv_h, wv)]
    routes = [
        local_copy(7, exp_a, exp_ref.at[0]),
        local_copy(8, exp_b, exp_ref.at[1]),
        local_copy(9, slot_a, slot_ref.at[0]),
        local_copy(10, slot_b, slot_ref.at[1]),
        local_copy(11, gate_a, gate_ref.at[0]),
        local_copy(12, gate_b, gate_ref.at[1]),
    ]
    load_out = local_copy(13, wo_h, wo)
    mine = pl.ds(0, local)
    theirs = pl.ds(local, local)
    ffn_loads = [local_copy(14, wg_h, wg.at[mine]), local_copy(15, wu_h, wu.at[mine]), local_copy(16, wd_h, wd.at[mine])]

    def rms(src_ref, gain_ref, put):
        gain = gain_ref[...].astype(F32)

        def strip(i, carry):
            rows = pl.ds(pl.multiple_of(i * 16, 16), 16)
            xs = src_ref[rows, :].astype(F32)
            inv = lax.rsqrt(jnp.mean(xs * xs, axis=-1, keepdims=True) + NORM_EPS)
            for j in range(blocks):
                put(i, j, (xs[:, j * LANES:(j + 1) * LANES] * inv * gain[j:j + 1, :]).astype(BF16))
            return carry

        lax.fori_loop(0, both // 16, strip, 0)

    for copy in small:
        copy.wait()

    def put_a(i, j, val):
        a_ref[pl.ds(pl.multiple_of(i * 16, 16), 16), j * LANES:(j + 1) * LANES] = val

    rms(x_ref, again_ref, put_a)
    wide = 256
    for load, w, dst in zip(loads, (wq, wk, wv), (q_ref, k_ref, v_ref)):
        load.wait()
        for n in range(dim // wide):
            cols = slice(n * wide, (n + 1) * wide)
            dst[:, cols] = lax.dot_general(a_ref[...], w[cols, :], NT, preferred_element_type=F32).astype(BF16)

    pl.semaphore_wait(barrier, 5)
    remote(wg_h, wg.at[theirs], wrecv.at[0], sibling)
    remote(wu_h, wu.at[theirs], wrecv.at[1], sibling)
    remote(wd_h, wd.at[theirs], wrecv.at[2], sibling)

    row = lax.broadcasted_iota(jnp.int32, (2 * both, both), 0)
    col = lax.broadcasted_iota(jnp.int32, (2 * both, both), 1)
    row = jnp.where(row >= both, row - both, row)
    allowed = (row >= col) & ((row >= seq) == (col >= seq))
    lane = lax.broadcasted_iota(jnp.int32, (both, LANES), 1)
    head_dim = LANES // 2
    scale = head_dim ** -0.5
    for p in range(dim // LANES):
        cols = slice(p * LANES, (p + 1) * LANES)
        qp = q_ref[:, cols].astype(F32)
        vp = v_ref[:, cols].astype(F32)
        low = lane < head_dim
        qq = jnp.concatenate([jnp.where(low, qp, 0.0), jnp.where(low, 0.0, qp)], axis=0).astype(BF16)
        vv = jnp.concatenate([jnp.where(low, vp, 0.0), jnp.where(low, 0.0, vp)], axis=0).astype(BF16)
        s = lax.dot_general(qq, k_ref[:, cols], NT, preferred_element_type=F32) * scale
        s = jnp.where(allowed, s, MASK_VALUE)
        e = jnp.exp(s - jnp.max(s, axis=-1, keepdims=True))
        prob = (e / jnp.sum(e, axis=-1, keepdims=True)).astype(BF16)
        pp = jnp.concatenate([prob[:both], prob[both:]], axis=1)
        c_ref[:, cols] = jnp.dot(pp, vv, preferred_element_type=F32).astype(BF16)

    load_out.wait()
    for n in range(dim // wide):
        cols = slice(n * wide, (n + 1) * wide)
        res = jnp.dot(c_ref[...], wo[:, cols], preferred_element_type=F32)
        h_ref[:, cols] = (x_ref[:, cols].astype(F32) + res).astype(BF16)

    for copy in routes:
        copy.wait()
    eid = lax.broadcasted_iota(jnp.int32, (gw_rows, LANES), 0)
    eid = jnp.where(lax.broadcasted_iota(jnp.int32, (gw_rows, LANES), 1) >= seq, eid + gw_rows, eid)
    for b in range(2):
        ids = jnp.where(slot_ref[b] >= 0, exp_ref[b], -1)
        ids = jnp.concatenate([ids, ids], axis=1)
        gts = gate_ref[b].astype(F32)
        gts = jnp.concatenate([gts, gts], axis=1)
        gw = jnp.zeros((gw_rows, LANES), F32)
        for j in range(top_k):
            gw = gw + jnp.where(ids[j:j + 1, :] == eid, gts[j:j + 1, :], 0.0)
        usend[b, pl.ds(urows, gw_rows), :] = gw.astype(BF16)

    def put_u(i, j, val):
        b = lax.div(i, seq // 16)
        r = lax.rem(i, seq // 16) * 16
        usend[b, pl.ds(pl.multiple_of(j * seq + r, 16), 16), :] = val

    rms(h_ref, mgain_ref, put_u)

    for b in range(2):
        for d in range(2):
            remote(usend.at[b], ulr.at[0, core, d], agrecv.at[0, core, d], 2 * toward[d] + b)
    remote(usend.at[other], uown, orecv.at[0], sibling)

    first = lax.rem(experts * z, gw_rows)
    upper = (experts * z) // gw_rows
    sel_row = lax.broadcasted_iota(jnp.int32, (gw_rows, experts * LANES), 0)
    sel_slot = lax.div(lax.broadcasted_iota(jnp.int32, (gw_rows, experts * LANES), 1), LANES)
    wanted = first + lax.rem(local * core + sel_slot, experts)
    sel_ref[...] = jnp.where(sel_row == wanted, 1.0, 0.0).astype(BF16)

    def gates_of(sub):
        packed = sub[pl.ds(urows, gw_rows), :]
        w = lax.dot_general(packed, sel_ref[...], TN, preferred_element_type=F32)
        return jnp.where(upper == 1, w[seq:], w[:seq])

    def expert_pair(sub0, sub1, dst):
        for i, sub in enumerate((sub0, sub1)):
            w = gates_of(sub)
            for k in range(experts):
                wbuf[k, i * seq:(i + 1) * seq, :] = w[:, k * LANES:(k + 1) * LANES]
        dst[...] = jnp.zeros(dst.shape, F32)

        def one(k, carry):
            rows = jnp.concatenate(
                [jnp.concatenate([sub[j * seq:(j + 1) * seq, :] for j in range(blocks)], axis=1) for sub in (sub0, sub1)], axis=0
            )
            for n in range(ffn // wide):
                cols = slice(n * wide, (n + 1) * wide)
                g = jnp.dot(rows, wg[k, :, cols], preferred_element_type=F32)
                up = jnp.dot(rows, wu[k, :, cols], preferred_element_type=F32)
                hid_ref[:, cols] = (jax.nn.silu(g) * up).astype(BF16)
            w = wbuf[k]
            for n in range(dim // wide):
                o = jnp.dot(hid_ref[...], wd[k, :, n * wide:(n + 1) * wide], preferred_element_type=F32)
                o = o.astype(BF16).astype(F32)
                for m in range(wide // LANES):
                    cols = slice(n * wide + m * LANES, n * wide + (m + 1) * LANES)
                    dst[:, cols] += jnp.where(w > 0.0, w * o[:, m * LANES:(m + 1) * LANES], 0.0)
            return carry

        lax.fori_loop(0, experts, one, 0)

    size = seq // PIECES

    def partial_of(d, c, k, g):
        if k == half:
            return pfar.at[pl.ds(c * seq + g * size, size)]
        return part.at[k - 1, c, pl.ds((1 - d) * seq + g * size, size)]

    def pass_on(d, c, k):
        for g in range(PIECES):
            src = partial_of(d, c, k, g)
            if k > 1:
                dst = rbuf.at[d, k - 2, c, pl.ds(g * size, size)]
                remote(src, dst, rsrecv.at[d, k - 2, c, g], 2 * toward[d] + core)
            else:
                dst = fin.at[core, d, pl.ds(g * size, size)]
                remote(src, dst, finrecv.at[core, d, g], 2 * toward[d] + c)

    def add_and_pass(d, c, k):
        for g in range(PIECES):
            got = rbuf.at[d, k - 1, c, pl.ds(g * size, size)]
            arrived(got, rsrecv.at[d, k - 1, c, g])
            mine_k = partial_of(d, c, k, g)
            mine_k[...] += got[...]
        pass_on(d, c, k)

    for h in range(half - 1):
        for c in range(2):
            for d in range(2):
                arrived(ulr.at[h, c, d], agrecv.at[h, c, d])
                if h + 1 < half - 1:
                    remote(ulr.at[h, c, d], ulr.at[h + 1, c, d], agrecv.at[h + 1, c, d], 2 * toward[d] + core)
                elif c == d:
                    remote(ulr.at[h, c, d], ufar.at[c], agrecv.at[h + 1, c, d], 2 * toward[d] + core)
            if h == 0 and c == 0:
                for copy in ffn_loads:
                    copy.wait()
                arrived(wg.at[theirs], wrecv.at[0])
                arrived(wu.at[theirs], wrecv.at[1])
                arrived(wd.at[theirs], wrecv.at[2])
            expert_pair(ulr.at[h, c, 0], ulr.at[h, c, 1], part.at[h, c])
    for d in range(2):
        pass_on(d, 1 - d, half - 1)
    for c in range(2):
        arrived(ufar.at[c], agrecv.at[half - 1, c, c])
    expert_pair(ufar.at[0], ufar.at[1], pfar)
    for d in range(2):
        pass_on(d, d, half)

    arrived(uown, orecv.at[0])
    expert_pair(usend.at[core], uown, pown)
    remote(pown.at[pl.ds(seq, seq)], ownr, orecv.at[1], sibling)

    for r in range(half - 1):
        for d in range(2):
            if half - 2 - r >= 1:
                add_and_pass(d, 1 - d, half - 2 - r)
        for d in range(2):
            add_and_pass(d, d, half - 1 - r)

    arrived(ownr, orecv.at[1])
    for b in range(2):
        for d in range(2):
            for g in range(PIECES):
                arrived(fin.at[b, d, pl.ds(g * size, size)], finrecv.at[b, d, g])
    for b, own in ((core, pown.at[pl.ds(0, seq)]), (other, ownr)):
        hrow = pl.ds(pl.multiple_of(b * seq, seq), seq)
        out_ref[b] = (h_ref[hrow, :].astype(F32) + (own[...] + (fin[b, 0] + fin[b, 1]))).astype(BF16)
    outs = [local_copy(0, out_ref.at[0], out_a), local_copy(1, out_ref.at[1], out_b)]
    for copy in outs:
        copy.wait()
    for copy in sends:
        copy.wait_send()


def solution(mesh):
    group = mesh.shape["ep"]
    row_spec = P(("dp", "ep"), None)
    full_spec = P(None, None, None)
    gain_spec = P(None)
    expert_spec = P("ep", None, None)
    in_specs = (row_spec,) * 8 + (gain_spec, full_spec, full_spec, full_spec, full_spec, gain_spec, expert_spec, expert_spec, expert_spec)

    def device_fn(tokens_a, experts_a, slots_a, gates_a, tokens_b, experts_b, slots_b, gates_b, attn_gain, w_query, w_key, w_value, w_out, moe_gain, w_gate, w_up, w_down):
        seq, dim = tokens_a.shape
        top_k = experts_a.shape[1]
        heads, head_dim = w_query.shape[1:]
        local, _, ffn = w_gate.shape
        half = group // 4
        both = 2 * seq
        urows = dim // LANES * seq
        urows_all = urows + local * group // 2

        def project(w):
            return w.transpose(1, 2, 0).reshape(heads * head_dim, dim)

        args = (
            tokens_a, experts_a.T, slots_a.T, gates_a.T, tokens_b, experts_b.T, slots_b.T, gates_b.T,
            attn_gain.reshape(dim // LANES, LANES), project(w_query), project(w_key), project(w_value),
            w_out.reshape(heads * head_dim, dim), moe_gain.reshape(dim // LANES, LANES), w_gate, w_up, w_down,
        )
        vmem = pltpu.VMEM
        scratch = [
            vmem((both, dim), BF16),
            vmem((2, top_k, seq), jnp.int32),
            vmem((2, top_k, seq), jnp.int32),
            vmem((2, top_k, seq), BF16),
            vmem((dim // LANES, LANES), BF16),
            vmem((dim // LANES, LANES), BF16),
            vmem((heads * head_dim, dim), BF16),
            vmem((heads * head_dim, dim), BF16),
            vmem((heads * head_dim, dim), BF16),
            vmem((heads * head_dim, dim), BF16),
            vmem((2 * local, dim, ffn), BF16),
            vmem((2 * local, dim, ffn), BF16),
            vmem((2 * local, ffn, dim), BF16),
            vmem((both, dim), BF16),
            vmem((both, dim), BF16),
            vmem((both, dim), BF16),
            vmem((both, dim), BF16),
            vmem((both, dim), BF16),
            vmem((both, dim), BF16),
            vmem((2, urows_all, LANES), BF16),
            vmem((urows_all, LANES), BF16),
            vmem((half - 1, 2, 2, urows_all, LANES), BF16),
            vmem((2, urows_all, LANES), BF16),
            vmem((local * group // 2, 2 * local * LANES), BF16),
            vmem((2 * local, both, LANES), F32),
            vmem((both, ffn), BF16),
            vmem((half - 1, 2, both, dim), F32),
            vmem((both, dim), F32),
            vmem((both, dim), F32),
            vmem((2, half - 1, 2, seq, dim), F32),
            vmem((2, 2, seq, dim), F32),
            vmem((seq, dim), F32),
            vmem((2, seq, dim), BF16),
            pltpu.SemaphoreType.DMA((17,)),
            pltpu.SemaphoreType.DMA((9 + 4 * (half - 2) + 2 + 1 + (2 * half - 1) * 2 * PIECES,)),
            pltpu.SemaphoreType.DMA((3,)),
            pltpu.SemaphoreType.DMA((2,)),
            pltpu.SemaphoreType.DMA((half, 2, 2)),
            pltpu.SemaphoreType.DMA((2, half - 1, 2, PIECES)),
            pltpu.SemaphoreType.DMA((2, 2, PIECES)),
        ]
        rows_all = group * seq
        return pl.pallas_call(
            functools.partial(layer_kernel, group),
            name="layer",
            out_shape=[jax.ShapeDtypeStruct((seq, dim), BF16)] * 2,
            in_specs=[pl.BlockSpec(memory_space=pl.ANY)] * len(args),
            out_specs=[pl.BlockSpec(memory_space=pl.ANY)] * 2,
            scratch_shapes=scratch,
            compiler_params=pltpu.CompilerParams(collective_id=0, has_side_effects=True, vmem_limit_bytes=60 * 1024 * 1024),
            cost_estimate=pl.CostEstimate(
                flops=rows_all * 6 * 2 * local * dim * ffn + both * 8 * dim * dim, bytes_accessed=2 * dim * (4 * dim + 3 * local * ffn), transcendentals=0
            ),
        )(*args)

    return jax.shard_map(device_fn, mesh=mesh, in_specs=in_specs, out_specs=(row_spec, row_spec), check_vma=False)
```

time: 267 us -> 88 us (0.33)
  waiting for transfers between devices: 148 us -> 0 us
  Pallas kernels: 0 us -> 84.1 us
  matrix products: 43.7 us -> 0 us
  local copies, waits for them, and re-layouts: 33.5 us -> 3.14 us
  starting transfers between devices: 27.3 us -> 0 us
  other arithmetic: 12.8 us -> 0 us
    all_to_all x4 -> x0, waiting for transfers between devices: 148 us -> none  [the longest x2 76 us: moe_layer(): returned = lax.all_to_all(expert_out, 'ep', 0, 0, tiled=True)]
    pallas_call x0 -> x1, Pallas kernels: none -> 84.1 us  [device_fn(): pl.pallas_call(functools.partial(layer_kernel, group), name='layer', out_...]
    dot_general x14 -> x0, matrix products: 43.7 us -> none  [the longest x2 13.5 us: expert_ffn(): jnp.einsum('pecf,efd->pecd', hidden, w_down, preferred_element_type=jnp.f...]
    all_to_all x4 -> x0, starting transfers between devices: 27.3 us -> none  [the longest x2 16.3 us: moe_layer(): lax.all_to_all(dispatched, 'ep', 0, 0, tiled=True)]
    gather x4 -> x0, local copies, waits for them, and re-layouts: 19.9 us -> none  [the longest x2 10.8 us: dispatch_rows(): jnp.take(normed, source, axis=0, mode='fill', fill_value=0)]
    select_n x9 -> x0, other arithmetic: 6.41 us -> none  [the longest x2 6.37 us: dispatch_rows(): jnp.take(normed, source, axis=0, mode='fill', fill_value=0)]
    convert_element_type x2 -> x0, local copies, waits for them, and re-layouts: 6.38 us -> none  [expert_ffn(): jnp.einsum('pecf,efd->pecd', hidden, w_down, preferred_element_type=jnp.f...]
    scatter x2 -> x0, local copies, waits for them, and re-layouts: 4.89 us -> none  [dispatch_rows(): jnp.full((experts_total * capacity,), seq_len, jnp.int32).at[dest_row]]
  transfers between devices with their start and end apart: 4 -> 0, of which waited for: 4 -> 0; matrix products, arithmetic and copies ran while one was open for 18% -> 0% of each run, Pallas kernels for 0% -> 0%
where the time goes in v1:
time: 88 us; the launch traced here: 87.9 us
  Pallas kernels  84.1 us (96%)
  local copies, waits for them, and re-layouts  3.14 us (4%)
    pallas_call x1, Pallas kernels, device_fn(): pl.pallas_call(functools.partial(layer_kernel, group), name='layer', out_...  84.1 us
    unnamed x2, local copies, waits for them, and re-layouts  3.14 us

profile of v1, /device:TPU:21, one launch (start us, length us, event | category | flops | bytes accessed | tf_op | source)
XLA Modules:
  0.0 87.9 jit_solution(11282693510251033982)
XLA Ops:
  0.6 84.1 %layer.1 = (bf16[64,1024]{1,0:T(8,128)(2,1)}, bf16[64,1024]{1,0:T(8,128)(2,1)}) custom-call(bf16[64,1024]{1,0:T(8,128)(2,1)} %tok_a.1, s32[8,64]{1,0:T(8,128)} %bitcast.22, s32[8,64]{1,0:T(8,128)} %bitcast.23, bf16[8,64]{1,0:T(8,128)(2,1)} %bitcast.26, bf16[64,1024]{1,0:T(8,128)(2,1)} %tok_b.1, s32[8,64]{1,0:T(8,128)} %bitcast.24, s32[8,64]{1,0:T(8,128)} %bitcast.25, ...), custom_call_target="tpu_custom_call" | custom-call | flops 13958643712 | bytes 14680064 | tf_op jit(solution)/shard_map/layer/pallas_call | solution.py:362
  84.7 1.6 %copy.21 = bf16[64,1024]{1,0:T(8,128)(2,1)} copy(bf16[64,1024]{1,0:T(8,128)(2,1)} %get-tuple-element.4) | data formatting | bytes 262144
  86.3 1.6 %copy.22 = bf16[64,1024]{1,0:T(8,128)(2,1)} copy(bf16[64,1024]{1,0:T(8,128)(2,1)} %get-tuple-element.5) | data formatting | bytes 262144

commit v2 on v1

--- a/solution.py
+++ b/solution.py
@@ -10,7 +10,7 @@
 NORM_EPS = 1e-6
 MASK_VALUE = -1e30
 LANES = 128
-PIECES = 1
+PIECES = 2
 MESH = pl.DeviceIdType.MESH
 NT = (((1,), (1,)), ((), ()))
 TN = (((0,), (0,)), ((), ()))
@@ -21,7 +21,7 @@
 def layer_kernel(
     group,
     tok_a, exp_a, slot_a, gate_a, tok_b, exp_b, slot_b, gate_b, attn_gain, wq_h, wk_h, wv_h, wo_h, moe_gain, wg_h, wu_h, wd_h,
-    out_a, out_b,
+    out,
     x_ref, exp_ref, slot_ref, gate_ref, again_ref, mgain_ref, wq, wk, wv, wo, wg, wu, wd,
     a_ref, q_ref, k_ref, v_ref, c_ref, h_ref, usend, uown, ulr, ufar, sel_ref, wbuf, hid_ref,
     part, pfar, pown, rbuf, fin, ownr, out_ref,
@@ -77,7 +77,9 @@
         local_copy(2, attn_gain, again_ref),
         local_copy(3, moe_gain, mgain_ref),
     ]
-    loads = [local_copy(4, wq_h, wq), local_copy(5, wk_h, wk), local_copy(6, wv_h, wv)]
+    parts = [pl.ds(i * (dim // 4), dim // 4) for i in range(4)]
+    loads = [[local_copy(17 + i, wq_h.at[rows], wq.at[rows]) for i, rows in enumerate(parts)]]
+    loads += [[local_copy(5, wk_h, wk)], [local_copy(6, wv_h, wv)]]
     routes = [
         local_copy(7, exp_a, exp_ref.at[0]),
         local_copy(8, exp_b, exp_ref.at[1]),
@@ -102,26 +104,27 @@
                 put(i, j, (xs[:, j * LANES:(j + 1) * LANES] * inv * gain[j:j + 1, :]).astype(BF16))
             return carry
 
-        lax.fori_loop(0, both // 16, strip, 0)
-
-    for copy in small:
-        copy.wait()
-
-    def put_a(i, j, val):
-        a_ref[pl.ds(pl.multiple_of(i * 16, 16), 16), j * LANES:(j + 1) * LANES] = val
-
-    rms(x_ref, again_ref, put_a)
-    wide = 256
-    for load, w, dst in zip(loads, (wq, wk, wv), (q_ref, k_ref, v_ref)):
-        load.wait()
-        for n in range(dim // wide):
-            cols = slice(n * wide, (n + 1) * wide)
-            dst[:, cols] = lax.dot_general(a_ref[...], w[cols, :], NT, preferred_element_type=F32).astype(BF16)
+        lax.fori_loop(0, both // 16, strip, 0, unroll=True)
 
     pl.semaphore_wait(barrier, 5)
     remote(wg_h, wg.at[theirs], wrecv.at[0], sibling)
     remote(wu_h, wu.at[theirs], wrecv.at[1], sibling)
     remote(wd_h, wd.at[theirs], wrecv.at[2], sibling)
+
+    for copy in small:
+        copy.wait()
+
+    def put_a(i, j, val):
+        a_ref[pl.ds(pl.multiple_of(i * 16, 16), 16), j * LANES:(j + 1) * LANES] = val
+
+    rms(x_ref, again_ref, put_a)
+    wide = 256
+    for load, w, dst in zip(loads, (wq, wk, wv), (q_ref, k_ref, v_ref)):
+        for n in range(dim // LANES):
+            if n % (dim // LANES // len(load)) == 0:
+                load[n // (dim // LANES // len(load))].wait()
+            cols = slice(n * LANES, (n + 1) * LANES)
+            dst[:, cols] = lax.dot_general(a_ref[...], w[cols, :], NT, preferred_element_type=F32).astype(BF16)
 
     row = lax.broadcasted_iota(jnp.int32, (2 * both, both), 0)
     col = lax.broadcasted_iota(jnp.int32, (2 * both, both), 1)
@@ -171,17 +174,20 @@
 
     rms(h_ref, mgain_ref, put_u)
 
-    for b in range(2):
-        for d in range(2):
-            remote(usend.at[b], ulr.at[0, core, d], agrecv.at[0, core, d], 2 * toward[d] + b)
+    def first_hop(b, d):
+        remote(usend.at[b], ulr.at[0, core, d], agrecv.at[0, core, d], 2 * jnp.where(d == 0, right, left) + b)
+
     remote(usend.at[other], uown, orecv.at[0], sibling)
-
+    first_hop(0, core)
+    first_hop(1, core)
     first = lax.rem(experts * z, gw_rows)
     upper = (experts * z) // gw_rows
     sel_row = lax.broadcasted_iota(jnp.int32, (gw_rows, experts * LANES), 0)
     sel_slot = lax.div(lax.broadcasted_iota(jnp.int32, (gw_rows, experts * LANES), 1), LANES)
     wanted = first + lax.rem(local * core + sel_slot, experts)
     sel_ref[...] = jnp.where(sel_row == wanted, 1.0, 0.0).astype(BF16)
+    first_hop(0, other)
+    first_hop(1, other)
 
     def gates_of(sub):
         packed = sub[pl.ds(urows, gw_rows), :]
@@ -193,86 +199,94 @@
             w = gates_of(sub)
             for k in range(experts):
                 wbuf[k, i * seq:(i + 1) * seq, :] = w[:, k * LANES:(k + 1) * LANES]
-        dst[...] = jnp.zeros(dst.shape, F32)
-
-        def one(k, carry):
-            rows = jnp.concatenate(
-                [jnp.concatenate([sub[j * seq:(j + 1) * seq, :] for j in range(blocks)], axis=1) for sub in (sub0, sub1)], axis=0
-            )
+        rows = jnp.concatenate(
+            [jnp.concatenate([sub[j * seq:(j + 1) * seq, :] for j in range(blocks)], axis=1) for sub in (sub0, sub1)], axis=0
+        )
+        for k in range(experts):
             for n in range(ffn // wide):
                 cols = slice(n * wide, (n + 1) * wide)
                 g = jnp.dot(rows, wg[k, :, cols], preferred_element_type=F32)
                 up = jnp.dot(rows, wu[k, :, cols], preferred_element_type=F32)
-                hid_ref[:, cols] = (jax.nn.silu(g) * up).astype(BF16)
-            w = wbuf[k]
-            for n in range(dim // wide):
-                o = jnp.dot(hid_ref[...], wd[k, :, n * wide:(n + 1) * wide], preferred_element_type=F32)
+                hid_ref[k, :, cols] = (jax.nn.silu(g) * up).astype(BF16)
+        for n in range(dim // wide):
+            total = None
+            for k in range(experts):
+                o = jnp.dot(hid_ref[k], wd[k, :, n * wide:(n + 1) * wide], preferred_element_type=F32)
                 o = o.astype(BF16).astype(F32)
-                for m in range(wide // LANES):
-                    cols = slice(n * wide + m * LANES, n * wide + (m + 1) * LANES)
-                    dst[:, cols] += jnp.where(w > 0.0, w * o[:, m * LANES:(m + 1) * LANES], 0.0)
-            return carry
-
-        lax.fori_loop(0, experts, one, 0)
+                w = wbuf[k]
+                term = jnp.concatenate(
+                    [jnp.where(w > 0.0, w * o[:, m * LANES:(m + 1) * LANES], 0.0) for m in range(wide // LANES)], axis=1
+                )
+                total = term if total is None else total + term
+            dst[:, n * wide:(n + 1) * wide] = total
 
     size = seq // PIECES
 
     def partial_of(d, c, k, g):
         if k == half:
             return pfar.at[pl.ds(c * seq + g * size, size)]
-        return part.at[k - 1, c, pl.ds((1 - d) * seq + g * size, size)]
-
-    def pass_on(d, c, k):
-        for g in range(PIECES):
-            src = partial_of(d, c, k, g)
-            if k > 1:
-                dst = rbuf.at[d, k - 2, c, pl.ds(g * size, size)]
-                remote(src, dst, rsrecv.at[d, k - 2, c, g], 2 * toward[d] + core)
-            else:
-                dst = fin.at[core, d, pl.ds(g * size, size)]
-                remote(src, dst, finrecv.at[core, d, g], 2 * toward[d] + c)
-
-    def add_and_pass(d, c, k):
-        for g in range(PIECES):
-            got = rbuf.at[d, k - 1, c, pl.ds(g * size, size)]
-            arrived(got, rsrecv.at[d, k - 1, c, g])
-            mine_k = partial_of(d, c, k, g)
-            mine_k[...] += got[...]
-        pass_on(d, c, k)
+        came = 1 - d
+        return part.at[k - 1, 0 if c == came else 1, pl.ds(came * seq + g * size, size)]
+
+    def pass_on(d, c, k, g):
+        src = partial_of(d, c, k, g)
+        if k > 1:
+            dst = rbuf.at[d, k - 2, c, pl.ds(g * size, size)]
+            remote(src, dst, rsrecv.at[d, k - 2, c, g], 2 * toward[d] + core)
+        else:
+            dst = fin.at[core, d, pl.ds(g * size, size)]
+            remote(src, dst, finrecv.at[core, d, g], 2 * toward[d] + c)
+
+    def add_and_pass(d, c, k, g):
+        got = rbuf.at[d, k - 1, c, pl.ds(g * size, size)]
+        arrived(got, rsrecv.at[d, k - 1, c, g])
+        mine_k = partial_of(d, c, k, g)
+        mine_k[...] += got[...]
+        pass_on(d, c, k, g)
+
+    both_ways = [(d, g) for g in range(PIECES) for d in range(2)]
 
     for h in range(half - 1):
-        for c in range(2):
+        for first_set in (True, False):
             for d in range(2):
+                c = d if first_set else 1 - d
                 arrived(ulr.at[h, c, d], agrecv.at[h, c, d])
                 if h + 1 < half - 1:
                     remote(ulr.at[h, c, d], ulr.at[h + 1, c, d], agrecv.at[h + 1, c, d], 2 * toward[d] + core)
-                elif c == d:
+                elif first_set:
                     remote(ulr.at[h, c, d], ufar.at[c], agrecv.at[h + 1, c, d], 2 * toward[d] + core)
-            if h == 0 and c == 0:
+            if h == 0:
+                if first_set:
+                    continue
                 for copy in ffn_loads:
                     copy.wait()
                 arrived(wg.at[theirs], wrecv.at[0])
                 arrived(wu.at[theirs], wrecv.at[1])
                 arrived(wd.at[theirs], wrecv.at[2])
-            expert_pair(ulr.at[h, c, 0], ulr.at[h, c, 1], part.at[h, c])
-    for d in range(2):
-        pass_on(d, 1 - d, half - 1)
+                expert_pair(ulr.at[h, 0, 0], ulr.at[h, 1, 1], part.at[h, 0])
+            if first_set:
+                expert_pair(ulr.at[h, 0, 0], ulr.at[h, 1, 1], part.at[h, 0])
+            else:
+                expert_pair(ulr.at[h, 1, 0], ulr.at[h, 0, 1], part.at[h, 1])
+            if h == half - 2 and first_set:
+                for d, g in both_ways:
+                    pass_on(d, 1 - d, half - 1, g)
     for c in range(2):
         arrived(ufar.at[c], agrecv.at[half - 1, c, c])
     expert_pair(ufar.at[0], ufar.at[1], pfar)
-    for d in range(2):
-        pass_on(d, d, half)
+    for d, g in both_ways:
+        pass_on(d, d, half, g)
 
     arrived(uown, orecv.at[0])
     expert_pair(usend.at[core], uown, pown)
     remote(pown.at[pl.ds(seq, seq)], ownr, orecv.at[1], sibling)
 
     for r in range(half - 1):
-        for d in range(2):
-            if half - 2 - r >= 1:
-                add_and_pass(d, 1 - d, half - 2 - r)
-        for d in range(2):
-            add_and_pass(d, d, half - 1 - r)
+        if half - 2 - r >= 1:
+            for d, g in both_ways:
+                add_and_pass(d, 1 - d, half - 2 - r, g)
+        for d, g in both_ways:
+            add_and_pass(d, d, half - 1 - r, g)
 
     arrived(ownr, orecv.at[1])
     for b in range(2):
@@ -282,9 +296,7 @@
     for b, own in ((core, pown.at[pl.ds(0, seq)]), (other, ownr)):
         hrow = pl.ds(pl.multiple_of(b * seq, seq), seq)
         out_ref[b] = (h_ref[hrow, :].astype(F32) + (own[...] + (fin[b, 0] + fin[b, 1]))).astype(BF16)
-    outs = [local_copy(0, out_ref.at[0], out_a), local_copy(1, out_ref.at[1], out_b)]
-    for copy in outs:
-        copy.wait()
+    local_copy(0, out_ref, out).wait()
     for copy in sends:
         copy.wait_send()
 
@@ -342,7 +354,7 @@
             vmem((2, urows_all, LANES), BF16),
             vmem((local * group // 2, 2 * local * LANES), BF16),
             vmem((2 * local, both, LANES), F32),
-            vmem((both, ffn), BF16),
+            vmem((2 * local, both, ffn), BF16),
             vmem((half - 1, 2, both, dim), F32),
             vmem((both, dim), F32),
             vmem((both, dim), F32),
@@ -350,7 +362,7 @@
             vmem((2, 2, seq, dim), F32),
             vmem((seq, dim), F32),
             vmem((2, seq, dim), BF16),
-            pltpu.SemaphoreType.DMA((17,)),
+            pltpu.SemaphoreType.DMA((21,)),
             pltpu.SemaphoreType.DMA((9 + 4 * (half - 2) + 2 + 1 + (2 * half - 1) * 2 * PIECES,)),
             pltpu.SemaphoreType.DMA((3,)),
             pltpu.SemaphoreType.DMA((2,)),
@@ -359,17 +371,18 @@
             pltpu.SemaphoreType.DMA((2, 2, PIECES)),
         ]
         rows_all = group * seq
-        return pl.pallas_call(
+        out = pl.pallas_call(
             functools.partial(layer_kernel, group),
             name="layer",
-            out_shape=[jax.ShapeDtypeStruct((seq, dim), BF16)] * 2,
+            out_shape=jax.ShapeDtypeStruct((2, seq, dim), BF16),
             in_specs=[pl.BlockSpec(memory_space=pl.ANY)] * len(args),
-            out_specs=[pl.BlockSpec(memory_space=pl.ANY)] * 2,
+            out_specs=pl.BlockSpec(memory_space=pl.ANY),
             scratch_shapes=scratch,
             compiler_params=pltpu.CompilerParams(collective_id=0, has_side_effects=True, vmem_limit_bytes=60 * 1024 * 1024),
             cost_estimate=pl.CostEstimate(
                 flops=rows_all * 6 * 2 * local * dim * ffn + both * 8 * dim * dim, bytes_accessed=2 * dim * (4 * dim + 3 * local * ffn), transcendentals=0
             ),
         )(*args)
+        return out[0], out[1]
 
     return jax.shard_map(device_fn, mesh=mesh, in_specs=in_specs, out_specs=(row_spec, row_spec), check_vma=False)

time: 88 us -> 78.9 us (0.90)
  Pallas kernels: 84.1 us -> 76.5 us
  local copies, waits for them, and re-layouts: 3.14 us -> 1.68 us
    pallas_call x1, Pallas kernels: 84.1 us -> 76.5 us  [device_fn(): pl.pallas_call(functools.partial(layer_kernel, group), name='layer', out_...]
    unnamed x2 -> x0, local copies, waits for them, and re-layouts: 3.14 us -> none
    squeeze x0 -> x1, local copies, waits for them, and re-layouts: none -> 1.68 us  [device_fn(): return (out[0], out[1])]
where the time goes in v2:
time: 78.9 us; the launch traced here: 78.8 us
  Pallas kernels  76.5 us (97%)
  local copies, waits for them, and re-layouts  1.68 us (2%)
    pallas_call x1, Pallas kernels, device_fn(): pl.pallas_call(functools.partial(layer_kernel, group), name='layer', out_...  76.5 us
    squeeze x1, local copies, waits for them, and re-layouts, device_fn(): return (out[0], out[1])  1.68 us

profile of v2, /device:TPU:21, one launch (start us, length us, event | category | flops | bytes accessed | tf_op | source)
XLA Modules:
  0.0 78.8 jit_solution(16140843519992588648)
XLA Ops:
  0.6 76.5 %layer.1 = bf16[2,64,1024]{2,1,0:T(8,128)(2,1)} custom-call(bf16[64,1024]{1,0:T(8,128)(2,1)} %tok_a.1, s32[8,64]{1,0:T(8,128)} %bitcast.26, s32[8,64]{1,0:T(8,128)} %bitcast.27, bf16[8,64]{1,0:T(8,128)(2,1)} %bitcast.30, bf16[64,1024]{1,0:T(8,128)(2,1)} %tok_b.1, s32[8,64]{1,0:T(8,128)} %bitcast.28, s32[8,64]{1,0:T(8,128)} %bitcast.29, ...), custom_call_target="tpu_custom_call" | custom-call | flops 13958643712 | bytes 14680064 | tf_op jit(solution)/shard_map/layer/pallas_call | solution.py:374
  77.1 1.7 %slice_bitcast_fusion = (bf16[64,1024]{1,0:T(8,128)(2,1)}, bf16[64,1024]{1,0:T(8,128)(2,1)}) fusion(bf16[2,64,1024]{2,1,0:T(8,128)(2,1)} %layer.1), kind=kLoop, calls=%fused_computation | loop fusion | bytes 524288 | tf_op jit(solution)/shard_map/squeeze | solution.py:386

commit v3 on v2

--- a/solution.py
+++ b/solution.py
@@ -23,8 +23,8 @@
     tok_a, exp_a, slot_a, gate_a, tok_b, exp_b, slot_b, gate_b, attn_gain, wq_h, wk_h, wv_h, wo_h, moe_gain, wg_h, wu_h, wd_h,
     out,
     x_ref, exp_ref, slot_ref, gate_ref, again_ref, mgain_ref, wq, wk, wv, wo, wg, wu, wd,
-    a_ref, q_ref, k_ref, v_ref, c_ref, h_ref, usend, uown, ulr, ufar, sel_ref, wbuf, hid_ref,
-    part, pfar, pown, rbuf, fin, ownr, out_ref,
+    a_ref, q_ref, k_ref, v_ref, c_ref, h_ref, htmp, xsend, utmp, usend, uown, ulr, ufar, sel_ref, wbuf, hid_ref,
+    part, pfar, pown, rbuf, fin, ownr,
     lsem, ssem, wrecv, orecv, agrecv, rsrecv, finrecv,
 ):
     seq, dim = tok_a.shape
@@ -71,15 +71,7 @@
             src_ref=dst, dst_ref=dst, send_sem=ssem.at[0], recv_sem=rsem, device_id={"ep": sibling}, device_id_type=MESH
         ).wait_recv()
 
-    small = [
-        local_copy(0, tok_a, x_ref.at[pl.ds(0, seq)]),
-        local_copy(1, tok_b, x_ref.at[pl.ds(seq, seq)]),
-        local_copy(2, attn_gain, again_ref),
-        local_copy(3, moe_gain, mgain_ref),
-    ]
-    parts = [pl.ds(i * (dim // 4), dim // 4) for i in range(4)]
-    loads = [[local_copy(17 + i, wq_h.at[rows], wq.at[rows]) for i, rows in enumerate(parts)]]
-    loads += [[local_copy(5, wk_h, wk)], [local_copy(6, wv_h, wv)]]
+    small = [local_copy(0, tok_a, x_ref.at[pl.ds(0, seq)]), local_copy(1, tok_b, x_ref.at[pl.ds(seq, seq)])]
     routes = [
         local_copy(7, exp_a, exp_ref.at[0]),
         local_copy(8, exp_b, exp_ref.at[1]),
@@ -87,25 +79,17 @@
         local_copy(10, slot_b, slot_ref.at[1]),
         local_copy(11, gate_a, gate_ref.at[0]),
         local_copy(12, gate_b, gate_ref.at[1]),
+        local_copy(2, attn_gain, again_ref),
+        local_copy(3, moe_gain, mgain_ref),
     ]
+    parts = [pl.ds(i * (dim // 4), dim // 4) for i in range(4)]
+    loads = [[local_copy(17 + i, wq_h.at[rows], wq.at[rows]) for i, rows in enumerate(parts)]]
+    loads += [[local_copy(5, wk_h, wk)], [local_copy(6, wv_h, wv)]]
     load_out = local_copy(13, wo_h, wo)
     mine = pl.ds(0, local)
     theirs = pl.ds(local, local)
     ffn_loads = [local_copy(14, wg_h, wg.at[mine]), local_copy(15, wu_h, wu.at[mine]), local_copy(16, wd_h, wd.at[mine])]
 
-    def rms(src_ref, gain_ref, put):
-        gain = gain_ref[...].astype(F32)
-
-        def strip(i, carry):
-            rows = pl.ds(pl.multiple_of(i * 16, 16), 16)
-            xs = src_ref[rows, :].astype(F32)
-            inv = lax.rsqrt(jnp.mean(xs * xs, axis=-1, keepdims=True) + NORM_EPS)
-            for j in range(blocks):
-                put(i, j, (xs[:, j * LANES:(j + 1) * LANES] * inv * gain[j:j + 1, :]).astype(BF16))
-            return carry
-
-        lax.fori_loop(0, both // 16, strip, 0, unroll=True)
-
     pl.semaphore_wait(barrier, 5)
     remote(wg_h, wg.at[theirs], wrecv.at[0], sibling)
     remote(wu_h, wu.at[theirs], wrecv.at[1], sibling)
@@ -113,46 +97,9 @@
 
     for copy in small:
         copy.wait()
-
-    def put_a(i, j, val):
-        a_ref[pl.ds(pl.multiple_of(i * 16, 16), 16), j * LANES:(j + 1) * LANES] = val
-
-    rms(x_ref, again_ref, put_a)
-    wide = 256
-    for load, w, dst in zip(loads, (wq, wk, wv), (q_ref, k_ref, v_ref)):
-        for n in range(dim // LANES):
-            if n % (dim // LANES // len(load)) == 0:
-                load[n // (dim // LANES // len(load))].wait()
-            cols = slice(n * LANES, (n + 1) * LANES)
-            dst[:, cols] = lax.dot_general(a_ref[...], w[cols, :], NT, preferred_element_type=F32).astype(BF16)
-
-    row = lax.broadcasted_iota(jnp.int32, (2 * both, both), 0)
-    col = lax.broadcasted_iota(jnp.int32, (2 * both, both), 1)
-    row = jnp.where(row >= both, row - both, row)
-    allowed = (row >= col) & ((row >= seq) == (col >= seq))
-    lane = lax.broadcasted_iota(jnp.int32, (both, LANES), 1)
-    head_dim = LANES // 2
-    scale = head_dim ** -0.5
-    for p in range(dim // LANES):
-        cols = slice(p * LANES, (p + 1) * LANES)
-        qp = q_ref[:, cols].astype(F32)
-        vp = v_ref[:, cols].astype(F32)
-        low = lane < head_dim
-        qq = jnp.concatenate([jnp.where(low, qp, 0.0), jnp.where(low, 0.0, qp)], axis=0).astype(BF16)
-        vv = jnp.concatenate([jnp.where(low, vp, 0.0), jnp.where(low, 0.0, vp)], axis=0).astype(BF16)
-        s = lax.dot_general(qq, k_ref[:, cols], NT, preferred_element_type=F32) * scale
-        s = jnp.where(allowed, s, MASK_VALUE)
-        e = jnp.exp(s - jnp.max(s, axis=-1, keepdims=True))
-        prob = (e / jnp.sum(e, axis=-1, keepdims=True)).astype(BF16)
-        pp = jnp.concatenate([prob[:both], prob[both:]], axis=1)
-        c_ref[:, cols] = jnp.dot(pp, vv, preferred_element_type=F32).astype(BF16)
-
-    load_out.wait()
-    for n in range(dim // wide):
-        cols = slice(n * wide, (n + 1) * wide)
-        res = jnp.dot(c_ref[...], wo[:, cols], preferred_element_type=F32)
-        h_ref[:, cols] = (x_ref[:, cols].astype(F32) + res).astype(BF16)
-
+    for b in range(2):
+        for j in range(blocks):
+            xsend[b, j * seq:(j + 1) * seq, :] = x_ref[b * seq:(b + 1) * seq, j * LANES:(j + 1) * LANES]
     for copy in routes:
         copy.wait()
     eid = lax.broadcasted_iota(jnp.int32, (gw_rows, LANES), 0)
@@ -165,42 +112,116 @@
         gw = jnp.zeros((gw_rows, LANES), F32)
         for j in range(top_k):
             gw = gw + jnp.where(ids[j:j + 1, :] == eid, gts[j:j + 1, :], 0.0)
+        xsend[b, pl.ds(urows, gw_rows), :] = gw.astype(BF16)
         usend[b, pl.ds(urows, gw_rows), :] = gw.astype(BF16)
 
-    def put_u(i, j, val):
-        b = lax.div(i, seq // 16)
-        r = lax.rem(i, seq // 16) * 16
-        usend[b, pl.ds(pl.multiple_of(j * seq + r, 16), 16), :] = val
-
-    rms(h_ref, mgain_ref, put_u)
-
-    def first_hop(b, d):
-        remote(usend.at[b], ulr.at[0, core, d], agrecv.at[0, core, d], 2 * jnp.where(d == 0, right, left) + b)
-
+    ways = (jnp.where(core == 0, right, left), jnp.where(core == 0, left, right))
+
+    def first_hop(src, b, d, way):
+        remote(src.at[b], ulr.at[0, core, d], agrecv.at[0, core, d], 2 * ways[way] + b)
+
+    first_hop(xsend, core, core, 0)
+    first_hop(xsend, other, core, 0)
+
+    wide = 256
+    row = lax.broadcasted_iota(jnp.int32, (2 * both, both), 0)
+    col = lax.broadcasted_iota(jnp.int32, (2 * both, both), 1)
+    row = jnp.where(row >= both, row - both, row)
+    allowed = (row >= col) & ((row >= seq) == (col >= seq))
+    low = lax.broadcasted_iota(jnp.int32, (both, LANES), 1) < LANES // 2
+    scale = (LANES // 2) ** -0.5
+
+    def scaled(xs, gain, j, inv):
+        return (xs[:, j * LANES:(j + 1) * LANES] * inv * gain[j:j + 1, :]).astype(BF16)
+
+    def attention(xs0, xs1, hdst, us0, us1, load=None, after_heads=None):
+        gain = again_ref[...].astype(F32)
+        for i in range(both // 16):
+            sub, r = (xs0, i * 16) if i * 16 < seq else (xs1, i * 16 - seq)
+            xs = jnp.concatenate([sub[pl.ds(j * seq + r, 16), :] for j in range(blocks)], axis=1).astype(F32)
+            inv = lax.rsqrt(jnp.mean(xs * xs, axis=-1, keepdims=True) + NORM_EPS)
+            for j in range(blocks):
+                a_ref[i * 16:(i + 1) * 16, j * LANES:(j + 1) * LANES] = scaled(xs, gain, j, inv)
+        for m, (w, dst) in enumerate(zip((wq, wk, wv), (q_ref, k_ref, v_ref))):
+            for n in range(dim // LANES):
+                if load is not None and n % (dim // LANES // len(load[m])) == 0:
+                    load[m][n // (dim // LANES // len(load[m]))].wait()
+                cols = slice(n * LANES, (n + 1) * LANES)
+                dst[:, cols] = lax.dot_general(a_ref[...], w[cols, :], NT, preferred_element_type=F32).astype(BF16)
+        for p in range(dim // LANES):
+            cols = slice(p * LANES, (p + 1) * LANES)
+            qp = q_ref[:, cols].astype(F32)
+            vp = v_ref[:, cols].astype(F32)
+            qq = jnp.concatenate([jnp.where(low, qp, 0.0), jnp.where(low, 0.0, qp)], axis=0).astype(BF16)
+            vv = jnp.concatenate([jnp.where(low, vp, 0.0), jnp.where(low, 0.0, vp)], axis=0).astype(BF16)
+            s = lax.dot_general(qq, k_ref[:, cols], NT, preferred_element_type=F32) * scale
+            s = jnp.where(allowed, s, MASK_VALUE)
+            e = jnp.exp(s - jnp.max(s, axis=-1, keepdims=True))
+            prob = (e / jnp.sum(e, axis=-1, keepdims=True)).astype(BF16)
+            pp = jnp.concatenate([prob[:both], prob[both:]], axis=1)
+            c_ref[:, cols] = jnp.dot(pp, vv, preferred_element_type=F32).astype(BF16)
+        if after_heads is not None:
+            after_heads()
+        if load is not None:
+            load_out.wait()
+        for n in range(dim // wide):
+            cols = slice(n * wide, (n + 1) * wide)
+            res = jnp.dot(c_ref[...], wo[:, cols], preferred_element_type=F32)
+            per = wide // LANES
+            xcols = jnp.concatenate(
+                [jnp.concatenate([sub[pl.ds((n * per + m) * seq, seq), :] for m in range(per)], axis=1) for sub in (xs0, xs1)], axis=0
+            )
+            hdst[:, cols] = (xcols.astype(F32) + res).astype(BF16)
+        gain = mgain_ref[...].astype(F32)
+        for i in range(both // 16):
+            sub, r = (us0, i * 16) if i * 16 < seq else (us1, i * 16 - seq)
+            xs = hdst[i * 16:(i + 1) * 16, :].astype(F32)
+            inv = lax.rsqrt(jnp.mean(xs * xs, axis=-1, keepdims=True) + NORM_EPS)
+            for j in range(blocks):
+                sub[pl.ds(j * seq + r, 16), :] = scaled(xs, gain, j, inv)
+
+    def forward(h, c, d, peer):
+        arrived(ulr.at[h, c, d], agrecv.at[h, c, d])
+        if h + 1 < half - 1:
+            remote(ulr.at[h, c, d], ulr.at[h + 1, c, d], agrecv.at[h + 1, c, d], 2 * peer + core)
+
+    def forward_x(h):
+        for d in range(2):
+            forward(h, d, d, toward[d])
+            if h + 1 == half - 1:
+                remote(ulr.at[h, d, d], ufar.at[d], agrecv.at[h + 1, d, d], 2 * toward[d] + core)
+
+    def forward_u(h):
+        for d in range(2):
+            forward(h, 1 - d, d, toward[d])
+
+    attention(
+        xsend.at[0], xsend.at[1], h_ref, usend.at[0], usend.at[1], loads, lambda: forward(0, core, core, ways[0])
+    )
+    forward(0, other, other, ways[1])
     remote(usend.at[other], uown, orecv.at[0], sibling)
-    first_hop(0, core)
-    first_hop(1, core)
+    first_hop(usend, 0, other, 1)
+    first_hop(usend, 1, other, 1)
+
     first = lax.rem(experts * z, gw_rows)
     upper = (experts * z) // gw_rows
     sel_row = lax.broadcasted_iota(jnp.int32, (gw_rows, experts * LANES), 0)
     sel_slot = lax.div(lax.broadcasted_iota(jnp.int32, (gw_rows, experts * LANES), 1), LANES)
     wanted = first + lax.rem(local * core + sel_slot, experts)
     sel_ref[...] = jnp.where(sel_row == wanted, 1.0, 0.0).astype(BF16)
-    first_hop(0, other)
-    first_hop(1, other)
 
     def gates_of(sub):
         packed = sub[pl.ds(urows, gw_rows), :]
         w = lax.dot_general(packed, sel_ref[...], TN, preferred_element_type=F32)
         return jnp.where(upper == 1, w[seq:], w[:seq])
 
-    def expert_pair(sub0, sub1, dst):
+    def expert_pair(us0, us1, sub0, sub1, dst):
         for i, sub in enumerate((sub0, sub1)):
             w = gates_of(sub)
             for k in range(experts):
                 wbuf[k, i * seq:(i + 1) * seq, :] = w[:, k * LANES:(k + 1) * LANES]
         rows = jnp.concatenate(
-            [jnp.concatenate([sub[j * seq:(j + 1) * seq, :] for j in range(blocks)], axis=1) for sub in (sub0, sub1)], axis=0
+            [jnp.concatenate([sub[j * seq:(j + 1) * seq, :] for j in range(blocks)], axis=1) for sub in (us0, us1)], axis=0
         )
         for k in range(experts):
             for n in range(ffn // wide):
@@ -246,42 +267,54 @@
 
     both_ways = [(d, g) for g in range(PIECES) for d in range(2)]
 
-    for h in range(half - 1):
-        for first_set in (True, False):
-            for d in range(2):
-                c = d if first_set else 1 - d
-                arrived(ulr.at[h, c, d], agrecv.at[h, c, d])
-                if h + 1 < half - 1:
-                    remote(ulr.at[h, c, d], ulr.at[h + 1, c, d], agrecv.at[h + 1, c, d], 2 * toward[d] + core)
-                elif first_set:
-                    remote(ulr.at[h, c, d], ufar.at[c], agrecv.at[h + 1, c, d], 2 * toward[d] + core)
-            if h == 0:
-                if first_set:
-                    continue
-                for copy in ffn_loads:
-                    copy.wait()
-                arrived(wg.at[theirs], wrecv.at[0])
-                arrived(wu.at[theirs], wrecv.at[1])
-                arrived(wd.at[theirs], wrecv.at[2])
-                expert_pair(ulr.at[h, 0, 0], ulr.at[h, 1, 1], part.at[h, 0])
-            if first_set:
-                expert_pair(ulr.at[h, 0, 0], ulr.at[h, 1, 1], part.at[h, 0])
-            else:
-                expert_pair(ulr.at[h, 1, 0], ulr.at[h, 0, 1], part.at[h, 1])
-            if h == half - 2 and first_set:
-                for d, g in both_ways:
-                    pass_on(d, 1 - d, half - 1, g)
+    def attention_x(h, after_heads=None):
+        attention(ulr.at[h, 0, 0], ulr.at[h, 1, 1], htmp, utmp.at[h, 0], utmp.at[h, 1], None, after_heads)
+
+    def experts_x(h):
+        expert_pair(utmp.at[h, 0], utmp.at[h, 1], ulr.at[h, 0, 0], ulr.at[h, 1, 1], part.at[h, 0])
+
+    def experts_u(h):
+        subs = (ulr.at[h, 1, 0], ulr.at[h, 0, 1])
+        expert_pair(*subs, *subs, part.at[h, 1])
+
+    last = half - 2
+    for h in range(last):
+        if h > 0:
+            forward_x(h)
+        attention_x(h, functools.partial(forward_u, h - 1) if h > 0 else None)
+        if h == last - 1:
+            for copy in ffn_loads:
+                copy.wait()
+            arrived(wg.at[theirs], wrecv.at[0])
+            arrived(wu.at[theirs], wrecv.at[1])
+            arrived(wd.at[theirs], wrecv.at[2])
+            experts_x(0)
+    forward_x(last)
+    attention_x(last, functools.partial(forward_u, last - 1))
+    experts_x(last)
+    for d, g in both_ways:
+        pass_on(d, 1 - d, half - 1, g)
     for c in range(2):
         arrived(ufar.at[c], agrecv.at[half - 1, c, c])
-    expert_pair(ufar.at[0], ufar.at[1], pfar)
+    attention(ufar.at[0], ufar.at[1], htmp, utmp.at[half - 1, 0], utmp.at[half - 1, 1])
+    expert_pair(utmp.at[half - 1, 0], utmp.at[half - 1, 1], ufar.at[0], ufar.at[1], pfar)
     for d, g in both_ways:
         pass_on(d, d, half, g)
-
+    for h in range(1, last):
+        experts_x(h)
+    for d, g in both_ways:
+        add_and_pass(d, 1 - d, half - 2, g)
+    forward_u(last)
+    experts_u(last)
+    for d, g in both_ways:
+        add_and_pass(d, d, half - 1, g)
+    for h in range(last):
+        experts_u(last - 1 - h)
     arrived(uown, orecv.at[0])
-    expert_pair(usend.at[core], uown, pown)
+    expert_pair(usend.at[core], uown, usend.at[core], uown, pown)
     remote(pown.at[pl.ds(seq, seq)], ownr, orecv.at[1], sibling)
 
-    for r in range(half - 1):
+    for r in range(1, half - 1):
         if half - 2 - r >= 1:
             for d, g in both_ways:
                 add_and_pass(d, 1 - d, half - 2 - r, g)
@@ -289,14 +322,14 @@
             add_and_pass(d, d, half - 1 - r, g)
 
     arrived(ownr, orecv.at[1])
-    for b in range(2):
-        for d in range(2):
-            for g in range(PIECES):
-                arrived(fin.at[b, d, pl.ds(g * size, size)], finrecv.at[b, d, g])
-    for b, own in ((core, pown.at[pl.ds(0, seq)]), (other, ownr)):
-        hrow = pl.ds(pl.multiple_of(b * seq, seq), seq)
-        out_ref[b] = (h_ref[hrow, :].astype(F32) + (own[...] + (fin[b, 0] + fin[b, 1]))).astype(BF16)
-    local_copy(0, out_ref, out).wait()
+    for g in range(PIECES):
+        rows = pl.ds(g * size, size)
+        for b in range(2):
+            for d in range(2):
+                arrived(fin.at[b, d, rows], finrecv.at[b, d, g])
+        for b, own in ((core, pown.at[rows]), (other, ownr.at[rows])):
+            hrow = pl.ds(pl.multiple_of(b * seq + g * size, size), size)
+            out[b, rows, :] = (h_ref[hrow, :].astype(F32) + (own[...] + (fin[b, 0, rows, :] + fin[b, 1, rows, :]))).astype(BF16)
     for copy in sends:
         copy.wait_send()
 
@@ -348,6 +381,9 @@
             vmem((both, dim), BF16),
             vmem((both, dim), BF16),
             vmem((both, dim), BF16),
+            vmem((both, dim), BF16),
+            vmem((2, urows_all, LANES), BF16),
+            vmem((half, 2, urows, LANES), BF16),
             vmem((2, urows_all, LANES), BF16),
             vmem((urows_all, LANES), BF16),
             vmem((half - 1, 2, 2, urows_all, LANES), BF16),
@@ -361,7 +397,6 @@
             vmem((2, half - 1, 2, seq, dim), F32),
             vmem((2, 2, seq, dim), F32),
             vmem((seq, dim), F32),
-            vmem((2, seq, dim), BF16),
             pltpu.SemaphoreType.DMA((21,)),
             pltpu.SemaphoreType.DMA((9 + 4 * (half - 2) + 2 + 1 + (2 * half - 1) * 2 * PIECES,)),
             pltpu.SemaphoreType.DMA((3,)),
@@ -374,9 +409,9 @@
         out = pl.pallas_call(
             functools.partial(layer_kernel, group),
             name="layer",
-            out_shape=jax.ShapeDtypeStruct((2, seq, dim), BF16),
+            out_shape=pltpu.VMEM((2, seq, dim), BF16),
             in_specs=[pl.BlockSpec(memory_space=pl.ANY)] * len(args),
-            out_specs=pl.BlockSpec(memory_space=pl.ANY),
+            out_specs=pl.BlockSpec(memory_space=pltpu.VMEM),
             scratch_shapes=scratch,
             compiler_params=pltpu.CompilerParams(collective_id=0, has_side_effects=True, vmem_limit_bytes=60 * 1024 * 1024),
             cost_estimate=pl.CostEstimate(

time: 78.9 us -> 73.8 us (0.935)
  Pallas kernels: 76.5 us -> 72.3 us
  local copies, waits for them, and re-layouts: 1.68 us -> 0.72 us
    pallas_call x1, Pallas kernels: 76.5 us -> 72.3 us  [device_fn(): pl.pallas_call(functools.partial(layer_kernel, group), name='layer', out_...]
    squeeze x1, local copies, waits for them, and re-layouts: 1.68 us -> 0.72 us  [device_fn(): return (out[0], out[1])]
where the time goes in v3:
time: 73.8 us; the launch traced here: 73.7 us
  Pallas kernels  72.3 us (98%)
    pallas_call x1, Pallas kernels, device_fn(): pl.pallas_call(functools.partial(layer_kernel, group), name='layer', out_...  72.3 us

profile of v3, /device:TPU:21, one launch (start us, length us, event | category | flops | bytes accessed | tf_op | source)
XLA Modules:
  0.0 73.7 jit_solution(13158393526535109148)
XLA Ops:
  0.6 72.3 %layer.1 = bf16[2,64,1024]{2,1,0:T(8,128)(2,1)S(1)} custom-call(bf16[64,1024]{1,0:T(8,128)(2,1)} %tok_a.1, s32[8,64]{1,0:T(8,128)} %bitcast.26, s32[8,64]{1,0:T(8,128)} %bitcast.27, bf16[8,64]{1,0:T(8,128)(2,1)} %bitcast.30, bf16[64,1024]{1,0:T(8,128)(2,1)} %tok_b.1, s32[8,64]{1,0:T(8,128)} %bitcast.28, s32[8,64]{1,0:T(8,128)} %bitcast.29, ...), custom_call_target="tpu_custom_call" | custom-call | flops 13958643712 | bytes 14680064 | tf_op jit(solution)/shard_map/layer/pallas_call | solution.py:409
  73.0 0.7 slice_bitcast_fusion

commit v4 on v3

--- a/solution.py
+++ b/solution.py
@@ -91,9 +91,6 @@
     ffn_loads = [local_copy(14, wg_h, wg.at[mine]), local_copy(15, wu_h, wu.at[mine]), local_copy(16, wd_h, wd.at[mine])]
 
     pl.semaphore_wait(barrier, 5)
-    remote(wg_h, wg.at[theirs], wrecv.at[0], sibling)
-    remote(wu_h, wu.at[theirs], wrecv.at[1], sibling)
-    remote(wd_h, wd.at[theirs], wrecv.at[2], sibling)
 
     for copy in small:
         copy.wait()
@@ -122,6 +119,9 @@
 
     first_hop(xsend, core, core, 0)
     first_hop(xsend, other, core, 0)
+    remote(wg_h, wg.at[theirs], wrecv.at[0], sibling)
+    remote(wu_h, wu.at[theirs], wrecv.at[1], sibling)
+    remote(wd_h, wd.at[theirs], wrecv.at[2], sibling)
 
     wide = 256
     row = lax.broadcasted_iota(jnp.int32, (2 * both, both), 0)

time: 73.8 us -> 73.8 us (level)
  no operation moved by 1% of the time
where the time goes in v4:
time: 73.8 us; the launch traced here: 73.7 us
  Pallas kernels  72.3 us (98%)
    pallas_call x1, Pallas kernels, device_fn(): pl.pallas_call(functools.partial(layer_kernel, group), name='layer', out_...  72.3 us

profile of v4, /device:TPU:21, one launch (start us, length us, event | category | flops | bytes accessed | tf_op | source)
XLA Modules:
  0.0 73.7 jit_solution(8175912055324675911)
XLA Ops:
  0.6 72.3 %layer.1 = bf16[2,64,1024]{2,1,0:T(8,128)(2,1)S(1)} custom-call(bf16[64,1024]{1,0:T(8,128)(2,1)} %tok_a.1, s32[8,64]{1,0:T(8,128)} %bitcast.26, s32[8,64]{1,0:T(8,128)} %bitcast.27, bf16[8,64]{1,0:T(8,128)(2,1)} %bitcast.30, bf16[64,1024]{1,0:T(8,128)(2,1)} %tok_b.1, s32[8,64]{1,0:T(8,128)} %bitcast.28, s32[8,64]{1,0:T(8,128)} %bitcast.29, ...), custom_call_target="tpu_custom_call" | custom-call | flops 13958643712 | bytes 14680064 | tf_op jit(solution)/shard_map/layer/pallas_call | solution.py:409
  73.0 0.7 slice_bitcast_fusion
